TPU v7x, 256 devices: a whole 4x4x8 slice. The times are simulated.
256 devices in a mesh: region: 128 (over z, y, x), level: 2 (over core).
Axes of the slice: x: 4, y: 4, z: 8, core: 2. Of those that a mesh axis runs over, the one named last changes fastest.
Arguments:
- latent: float32 [851968, 512], P('region', 'level'), may hold values from -6 to 6
- new_owner: int32 [6656], P('region'), may hold values from 0 to 127, as said below
- dest_slot: int32 [6656], P('region'), may hold values from 0 to 77, as said below
- live_rows: int32 [6656], P('region'), may hold values from 1 to 128
- norm_gain: float32 [512], P('level'), may hold values from 0.25 to 1.75
- w_in: bfloat16 [512, 512], replicated, may hold values from -0.25 to 0.25
- b_in: float32 [512], replicated, may hold values from -3 to 3
- w_out: bfloat16 [512, 512], P(None, 'level'), may hold values from -0.25 to 0.25
- b_out: float32 [512], P('level'), may hold values from -3 to 3
Outputs:
- updated: bfloat16 [1277952, 512], P('region', 'level')
Inputs may be any that keep to these rules, and one draw needn't show every extreme that they name: `new_owner`: A region receives at most 78 blocks and one region hands at most 1 of its blocks to one region; both bounds are reached in every draw. `dest_slot`: blocks with the same new owner have different slots.
All inputs are finite; a program needn't handle non-finite values.
Results may differ from a plain program's by a relative error of at most 0.0045.
Values may be sent and summed in bfloat16 or wider, within the bound.
No kernel may reach another device: no remote copies, remote signals or barrier semaphores. Data moves between devices by JAX's collectives and lax.ppermute only.
A program may use at most 128 MiB of HBM per device.

v0:
```python
import jax
import jax.numpy as jnp
from jax import lax
from jax.sharding import PartitionSpec as P

epsilon = 1e-05


def sent_to_all(x, axis):
    length = lax.axis_size(axis)
    return lax.all_to_all(jnp.broadcast_to(x[None], (length, *x.shape)), axis, 0, 0, tiled=True)


def taken_together(x, axis):
    return sent_to_all(x, axis).sum(axis=0)


def packed_total(arrays, axis):
    flat, at, done = (jnp.concatenate([a.reshape(-1) for a in arrays]), 0, [])
    subtotal = taken_together(flat, axis)
    for a in arrays:
        done.append(subtotal[at : at + a.size].reshape(a.shape))
        at += a.size
    return tuple(done)


def node_update(inputs, live, block_rows, norm_gain, w_in, b_in, w_out, b_out):
    width = w_in.shape[0]
    row_sums, row_squares = packed_total(
        (jnp.sum(inputs, axis=1), jnp.sum(inputs * inputs, axis=1)), "level"
    )
    average = row_sums / width
    variance = row_squares / width - average * average
    half_normed = (
        (inputs - average[:, None]) * lax.rsqrt(variance + epsilon)[:, None] * norm_gain
    ).astype(jnp.bfloat16)
    normed = lax.all_gather(half_normed, "level", axis=1, tiled=True)
    preact = jnp.dot(normed, w_in, preferred_element_type=jnp.float32) + b_in
    hidden = jax.nn.silu(preact).astype(jnp.bfloat16)
    result = jnp.dot(hidden, w_out, preferred_element_type=jnp.float32) + b_out + inputs
    keeping = (jnp.arange(block_rows, dtype=jnp.int32)[None, :] < live[:, None]).reshape(-1)
    return jnp.where(keeping[:, None], result, 0.0).astype(jnp.bfloat16)


def shards(latent, new_owner, dest_slot, live_rows, norm_gain, w_in, b_in, w_out, b_out):
    region_count = lax.axis_size("region")
    old_blocks = new_owner.shape[0]
    block_rows = latent.shape[0] // old_blocks
    half_width = latent.shape[1]
    slot_count = old_blocks + old_blocks // 2
    peer_slots = max(1, (slot_count + region_count - 1) // region_count)
    send_count = region_count * peer_slots
    counter = jnp.arange(old_blocks, dtype=jnp.int32)
    earlier = (new_owner[:, None] == new_owner[None, :]) & (counter[None, :] < counter[:, None])
    ranking = jnp.sum(earlier.astype(jnp.int32), axis=1)
    position = new_owner * peer_slots + ranking
    send_slots = jnp.full((send_count,), slot_count, jnp.int32).at[position].set(dest_slot)
    finished = node_update(latent, live_rows, block_rows, norm_gain, w_in, b_in, w_out, b_out)
    finished = finished.reshape(old_blocks, block_rows, half_width)
    send_data = (
        jnp.zeros((send_count, block_rows, half_width), jnp.bfloat16).at[position].set(finished)
    )
    got_data, got_slots = (
        lax.all_to_all(send_data, "region", split_axis=0, concat_axis=0, tiled=True),
        lax.all_to_all(send_slots, "region", split_axis=0, concat_axis=0, tiled=True),
    )
    arrived = (
        jnp.zeros((slot_count, block_rows, half_width), jnp.bfloat16)
        .at[got_slots]
        .set(got_data, mode="drop")
    )
    return arrived.reshape(slot_count * block_rows, half_width)


def solution(mesh):
    placed = (
        P("region", "level"),
        P("region"),
        P("region"),
        P("region"),
        P("level"),
        P(),
        P(),
        P(None, "level"),
        P("level"),
    )
    return jax.shard_map(
        shards, mesh=mesh, in_specs=placed, out_specs=P("region", "level"), check_vma=False
    )
```

profile of v0, /device:TPU:1, one launch (start us, length us, event | category | flops | bytes accessed | tf_op | source)
XLA Modules:
  0.0 308.5 jit_solution(12394421436280195811)
XLA Ops:
  6.5 0.0 copy-start
  6.5 0.0 copy-start.1
  6.5 0.0 all-gather.2.cloned.1.call-start
  6.5 4.8 %fusion.14 = (f32[6656]{0:T(1024)S(1)}, f32[6656]{0:T(1024)S(1)}) fusion(f32[6656,256]{1,0:T(8,128)} %param.9), kind=kLoop, calls=%fused_computation.29 | loop fusion | flops 5098496 | bytes 6868992 | tf_op jit(solution)/shard_map/reduce_sum | solution.py:30
  11.4 0.1 broadcast_in_dim.20
  11.5 6.7 %all_to_all.23 = f32[2,1,13312]{2,1,0:T(1,128)S(1)} all-to-all(f32[2,1,13312]{2,1,0:T(1,128)S(1)} %broadcast_in_dim.20), channel_id=1, replica_groups=mesh['region'=128,'level'=2] {'level'}, dimensions={0} | all-to-all | bytes 212992 | tf_op jit(solution)/shard_map/all_to_all | solution.py:11
  18.1 0.1 reduce_sum.39
  18.3 0.0 copy-done.1
  18.3 0.0 copy-start.6
  18.3 0.0 copy-start.2
  18.3 0.0 copy-start.3
  18.3 0.0 copy-start.4
  18.3 0.0 copy-start.5
  18.4 7.1 %multiply_convert_fusion.1 = bf16[6656,256]{1,0:T(8,128)(2,1)} fusion(f32[6656,256]{1,0:T(8,128)} %param.9, f32[256]{0:T(256)S(1)} %copy-done.1, f32[6656]{0:T(1024)S(1)} %get-tuple-element.8, f32[6656]{0:T(1024)S(1)} %get-tuple-element.7), kind=kLoop, calls=%fused_computation.10 | loop fusion | flops 6815744 | bytes 10277888 | tf_op jit(solution)/shard_map/convert_element_type | solution.py:36
  25.4 0.0 all-gather.2.cloned.1.call-update
  25.4 0.0 copy-done.6
  25.5 0.2 convert_reduce_fusion
  25.6 0.9 scatter_custom_fusion
  26.5 0.7 copy.13
  27.3 13.8 %all-to-all-start = ((s32[128,1,1]{2,1,0:T(1,128)}), s32[128,1,1]{2,1,0:T(1,128)S(1)}, u32[]{:S(2)}, u32[]{:S(2)}) async-start(s32[128,1,1]{2,1,0:T(1,128)} %copy.13), calls=%async_computation | async-start | bytes 131072 | tf_op jit(solution)/shard_map/all_to_all | solution.py:65
  41.1 0.0 copy-done.2
  41.1 0.1 fusion.9
  41.1 7.5 %all-gather.2.cloned.1.call-done = bf16[6656,512]{1,0:T(8,128)(2,1)} async-done(((bf16[6656,256]{1,0:T(8,128)(2,1)}), bf16[6656,512]{1,0:T(8,128)(2,1)}) %all-gather.2.cloned.1.call-update) | async-done | bytes 6815760 | tf_op jit(solution)/shard_map/all_gather | solution.py:37
  48.7 0.0 copy-done
  48.7 0.0 copy-done.3
  48.7 0.0 copy-done.4
  48.7 0.0 copy-done.5
  48.7 11.6 %fusion.2 = bf16[6656,256]{1,0:T(8,128)(2,1)} fusion(f32[6656,256]{1,0:T(8,128)} %param.9, bf16[512,256]{1,0:T(8,128)(2,1)S(1)} %copy-done.3, bf16[6656,512]{1,0:T(8,128)(2,1)} %all-gather.2.cloned.1.call-done, bf16[512,512]{1,0:T(8,128)(2,1)S(1)} %copy-done, f32[512]{0:T(512)S(1)} %copy-done.4, f32[256]{0:T(256)S(1)} %copy-done.5, ...), kind=kOutput, calls=%fused_computation.7 | convolution fusion | flops 5261754368 | bytes 17835520 | tf_op jit(solution)/shard_map/dot_general | solution.py:40
  60.3 4.3 %broadcast_in_dim.18 = bf16[128,128,256]{2,1,0:T(8,128)(2,1)} broadcast(bf16[]{:T(256)} %constant.8.clone.1), dimensions={} | broadcast | bytes 8388610 | tf_op jit(solution)/shard_map/broadcast_in_dim | solution.py:61
  64.5 11.8 %scatter_fusion = bf16[128,128,256]{2,1,0:T(8,128)(2,1)} fusion(bf16[128,128,256]{2,1,0:T(8,128)(2,1)} %broadcast_in_dim.18, s32[52]{0:T(128)S(1)} %compare_select_fusion.1, bf16[52,128,256]{2,1,0:T(8,128)(2,1)} %bitcast.12), kind=kCustom, calls=%fused_computation.1 | custom fusion | bytes 10223824 | tf_op jit(solution)/shard_map/scatter | solution.py:61
  76.4 0.0 all-to-all-done
  76.4 14.0 %all-to-all-start.2 = ((bf16[128,128,256]{2,1,0:T(8,128)(2,1)}), bf16[128,128,256]{2,1,0:T(8,128)(2,1)}, u32[]{:S(2)}, u32[]{:S(2)}) async-start(bf16[128,128,256]{2,1,0:T(8,128)(2,1)} %scatter_fusion), calls=%async_computation.2 | async-start | bytes 16777216 | tf_op jit(solution)/shard_map/all_to_all | solution.py:64
  90.3 2.4 reduce.1
  92.7 184.6 %all-to-all-done.2 = bf16[128,128,256]{2,1,0:T(8,128)(2,1)} async-done(((bf16[128,128,256]{2,1,0:T(8,128)(2,1)}), bf16[128,128,256]{2,1,0:T(8,128)(2,1)}, u32[]{:S(2)}, u32[]{:S(2)}) %all-to-all-start.2) | async-done | bytes 8388640 | tf_op jit(solution)/shard_map/all_to_all | solution.py:64
  277.3 2.9 broadcast_in_dim.16
  280.3 21.4 %scatter_fusion.1 = bf16[78,128,256]{2,1,0:T(8,128)(2,1)} fusion(bf16[78,128,256]{2,1,0:T(8,128)(2,1)} %broadcast_in_dim.16, s32[128]{0:T(128)S(1)} %fusion.10, bf16[128,128,256]{2,1,0:T(8,128)(2,1)} %all-to-all-done.2), kind=kCustom, calls=%fused_computation.2 | custom fusion | bytes 25166336 | tf_op jit(solution)/shard_map/scatter | solution.py:70
  (4 shorter events, 0.0 us)
Async XLA Ops:
  6.5 42.2 %copy-start = (bf16[512,512]{1,0:T(8,128)(2,1)S(1)}, bf16[512,512]{1,0:T(8,128)(2,1)}, u32[]{:S(2)}) copy-start(bf16[512,512]{1,0:T(8,128)(2,1)} %param.14) | copy-start | bytes 1572868
  6.5 11.8 %copy-start.1 = (f32[256]{0:T(256)S(1)}, f32[256]{0:T(256)}, u32[]{:S(2)}) copy-start(f32[256]{0:T(256)} %param.13) | copy-start | bytes 3076
  6.5 42.1 %all-gather.2.cloned.1.call-start = ((), (), s32[]{:S(2)}) async-start(), calls=%async_computation.3 | async-start | bytes 10223616 | tf_op jit(solution)/shard_map/all_gather | solution.py:37
  18.3 7.1 %copy-start.6 = (s32[52]{0:T(128)S(1)}, s32[52]{0:T(128)}, u32[]{:S(2)}) copy-start(s32[52]{0:T(128)} %param.10) | copy-start | bytes 628
  18.3 22.8 %copy-start.2 = (s32[52]{0:T(128)S(1)}, s32[52]{0:T(128)}, u32[]{:S(2)}) copy-start(s32[52]{0:T(128)} %param.12) | copy-start | bytes 628
  18.3 30.4 %copy-start.3 = (bf16[512,256]{1,0:T(8,128)(2,1)S(1)}, bf16[512,256]{1,0:T(8,128)(2,1)}, u32[]{:S(2)}) copy-start(bf16[512,256]{1,0:T(8,128)(2,1)} %param.16) | copy-start | bytes 786436
  18.3 30.4 %copy-start.4 = (f32[512]{0:T(512)S(1)}, f32[512]{0:T(512)}, u32[]{:S(2)}) copy-start(f32[512]{0:T(512)} %param.15) | copy-start | bytes 6148
  18.3 30.4 %copy-start.5 = (f32[256]{0:T(256)S(1)}, f32[256]{0:T(256)}, u32[]{:S(2)}) copy-start(f32[256]{0:T(256)} %param.17) | copy-start | bytes 3076
  27.3 49.1 %all-to-all-start = ((s32[128,1,1]{2,1,0:T(1,128)}), s32[128,1,1]{2,1,0:T(1,128)S(1)}, u32[]{:S(2)}, u32[]{:S(2)}) async-start(s32[128,1,1]{2,1,0:T(1,128)} %copy.13), calls=%async_computation | async-start | bytes 131072 | tf_op jit(solution)/shard_map/all_to_all | solution.py:65
  76.4 201.0 %all-to-all-start.2 = ((bf16[128,128,256]{2,1,0:T(8,128)(2,1)}), bf16[128,128,256]{2,1,0:T(8,128)(2,1)}, u32[]{:S(2)}, u32[]{:S(2)}) async-start(bf16[128,128,256]{2,1,0:T(8,128)(2,1)} %scatter_fusion), calls=%async_computation.2 | async-start | bytes 16777216 | tf_op jit(solution)/shard_map/all_to_all | solution.py:64
Sparse Core Ops, SparseCore 0:
  25.6 23.0 all-gather.1
where the time goes:
time: 310 us; the launch traced here: 308 us
  waiting for transfers between devices  192 us (62%)
  local copies, waits for them, and re-layouts  42.1 us (14%)
  starting transfers between devices  27.8 us (9%)
  other arithmetic  14.7 us (5%)
  between operations  13.5 us (4%)
  matrix products  11.6 us (4%)
  blocking collectives  6.66 us (2%)
    all_to_all x1, waiting for transfers between devices, shards(): lax.all_to_all(send_data, 'region', split_axis=0, concat_axis=0, tiled=True)  185 us
    scatter x1, local copies, waits for them, and re-layouts, shards(): arrived = jnp.zeros((slot_count, block_rows, half_width), jnp.bfloat16).a...  21.4 us
    all_to_all x1, starting transfers between devices, shards(): lax.all_to_all(send_data, 'region', split_axis=0, concat_axis=0, tiled=True)  14 us
    all_to_all x1, starting transfers between devices, shards(): lax.all_to_all(send_slots, 'region', split_axis=0, concat_axis=0, tiled=T...  13.8 us
    scatter x1, local copies, waits for them, and re-layouts, shards(): jnp.zeros((send_count, block_rows, half_width), jnp.bfloat16).at[position]  11.8 us
    dot_general x1, matrix products, node_update(): jnp.dot(hidden, w_out, preferred_element_type=jnp.float32) + b_out + inputs  11.6 us
    all_gather x1, waiting for transfers between devices, node_update(): normed = lax.all_gather(half_normed, 'level', axis=1, tiled=True)  7.55 us
    convert_element_type x1, other arithmetic, node_update(): half_normed = ((inputs - average[:, None]) * lax.rsqrt(variance + epsilon...  7.06 us
  transfers between devices with their start and end apart: 3, of which 2 were waited for; matrix products, arithmetic and copies ran while one was open for 10% of the time, Pallas kernels for 0%

commit v1 on v0

v1 whole, which is shorter than its diff:
```python
import functools

import jax
import jax.numpy as jnp
from jax import lax
from jax.experimental import pallas as pl
from jax.experimental.pallas import tpu as pltpu
from jax.sharding import PartitionSpec as P


epsilon = 1e-05
TILE = 16
PLANE = 16
CUTS = (0, 3, 6, 8)
FIRST = (27, 25, 15)
SECOND = (15, 15, 12)


def starts(sizes):
    out, at = [], 0
    for size in sizes:
        out.append(at)
        at += size
    return out


def mlp_kernel(level_ref, live_ref, mine_ref, theirs_ref, side_mine_ref, side_theirs_ref, w_in_ref,
               b_in_ref, w_mine_ref, w_theirs_ref, out_mine_ref, out_theirs_ref, *, block_rows, blocks, half_blocks):
    step = pl.program_id(0)
    level = level_ref[0]
    half = mine_ref.shape[1]
    mine, theirs = mine_ref[...], theirs_ref[...]
    width = 2 * half
    average = jnp.sum(mine + theirs, axis=1, keepdims=True) / width
    variance = jnp.sum(mine * mine + theirs * theirs, axis=1, keepdims=True) / width - average * average
    scale = lax.rsqrt(variance + epsilon)
    norm_mine = ((mine - average) * scale * side_mine_ref[0:1]).astype(jnp.bfloat16)
    norm_theirs = ((theirs - average) * scale * side_theirs_ref[0:1]).astype(jnp.bfloat16)
    at_mine = pl.multiple_of(level * half, half)
    at_theirs = pl.multiple_of((1 - level) * half, half)
    preact = (
        jnp.dot(norm_mine, w_in_ref[pl.ds(at_mine, half), :], preferred_element_type=jnp.float32)
        + jnp.dot(norm_theirs, w_in_ref[pl.ds(at_theirs, half), :], preferred_element_type=jnp.float32)
        + b_in_ref[...]
    )
    hidden = (preact / (1.0 + jnp.exp(-preact))).astype(jnp.bfloat16)
    row = lax.broadcasted_iota(jnp.int32, (block_rows, 1), 0)
    keeping = jnp.concatenate(
        [row < live_ref[level * half_blocks + step * blocks + i] for i in range(blocks)], axis=0
    )
    for w_ref, side_ref, rows, out_ref in (
        (w_mine_ref, side_mine_ref, mine, out_mine_ref),
        (w_theirs_ref, side_theirs_ref, theirs, out_theirs_ref),
    ):
        result = jnp.dot(hidden, w_ref[...], preferred_element_type=jnp.float32) + side_ref[1:2] + rows
        out_ref[...] = jnp.where(keeping, result, 0.0).astype(jnp.bfloat16)


def node_update(latent, live, norm_gain, w_in, b_in, w_out, b_out, old_blocks, block_rows):
    level = lax.axis_index("level")
    half_blocks = old_blocks // 2
    half_rows = half_blocks * block_rows
    width, half = latent.shape[1] * 2, latent.shape[1]
    hidden_width = w_in.shape[1]
    swap = [(0, 1), (1, 0)]
    sides = jnp.stack([norm_gain, b_out])
    going = lax.dynamic_slice_in_dim(latent, (1 - level) * half_rows, half_rows, 0)
    theirs = lax.ppermute(going, "level", swap)
    w_theirs = lax.ppermute(w_out, "level", swap)
    side_theirs = lax.ppermute(sides, "level", swap)
    blocks = 2
    rows = blocks * block_rows
    steps = half_rows // rows
    whole = lambda *shape: pl.BlockSpec(shape, lambda i, level_ref, live_ref: (0,) * len(shape))
    mlp = pl.pallas_call(
        functools.partial(mlp_kernel, block_rows=block_rows, blocks=blocks, half_blocks=half_blocks),
        grid_spec=pltpu.PrefetchScalarGridSpec(
            num_scalar_prefetch=2,
            grid=(steps,),
            in_specs=[
                pl.BlockSpec((rows, half), lambda i, level_ref, live_ref: (level_ref[0] * steps + i, 0)),
                pl.BlockSpec((rows, half), lambda i, level_ref, live_ref: (i, 0)),
                whole(2, half),
                whole(2, half),
                whole(width, hidden_width),
                whole(1, hidden_width),
                whole(hidden_width, half),
                whole(hidden_width, half),
            ],
            out_specs=[
                pl.BlockSpec((rows, half), lambda i, level_ref, live_ref: (i, 0)),
                pl.BlockSpec((rows, half), lambda i, level_ref, live_ref: (i, 0)),
            ],
        ),
        out_shape=[jax.ShapeDtypeStruct((half_rows, half), jnp.bfloat16)] * 2,
        name="node_mlp",
    )
    out_mine, out_theirs = mlp(level[None], live, latent, theirs, sides, side_theirs, w_in, b_in[None], w_out, w_theirs)
    return out_mine, lax.ppermute(out_theirs, "level", swap)


def plan_kernel(where_ref, table_ref, own_ref, fits_ref, pack_ref, relay_ref, place_ref, pos_ref, goal_ref):
    spot, depth = where_ref[0], where_ref[1]
    lanes = table_ref.shape[1]
    planes = lanes // PLANE
    tiles = 8
    total = sum(FIRST)
    f32, bf16 = jnp.float32, jnp.bfloat16
    table = table_ref[...]
    count = (table & 15).astype(f32)
    slot = (table >> 4).astype(f32)
    i0 = lax.broadcasted_iota(jnp.int32, (lanes, lanes), 0)
    i1 = lax.broadcasted_iota(jnp.int32, (lanes, lanes), 1)
    one = lambda mask: jnp.where(mask, 1.0, 0.0).astype(bf16)
    same = one(i0 // PLANE == i1 // PLANE)
    before = one((i0 // PLANE == i1 // PLANE) & (i0 < i1))
    above = one((i0 // planes == i1 // planes) & (i1 < i0))
    dot = lambda a, b: jnp.dot(a.astype(bf16), b.astype(bf16), preferred_element_type=f32)
    firsts, seconds = starts(FIRST), starts(SECOND)
    parts = range(len(FIRST))
    part_of = [c for c in parts for _ in range(CUTS[c], CUTS[c + 1])]
    fits = None
    run = []
    for c in parts:
        held = jnp.clip(count - CUTS[c], 0.0, float(CUTS[c + 1] - CUTS[c]))
        load = jnp.sum(held.reshape(lanes // planes, planes, lanes), axis=1)
        good = (jnp.max(dot(held, same)) <= FIRST[c]) & (jnp.max(load) <= SECOND[c])
        fits = good if fits is None else fits & good
        run.append(dot(above, held))
    fits_ref[0] = jnp.where(fits, 1, 0)
    lane = lax.broadcasted_iota(jnp.int32, (1, lanes), 1)
    within = (lane % PLANE).astype(f32)
    me = depth * PLANE + spot
    placed = jnp.zeros((lanes, lanes), f32)
    slot_col = jnp.sum(jnp.where(i1 == me, slot, 0.0), axis=1, keepdims=True)
    lane_f = i1.astype(f32)
    for t in range(tiles):
        c = part_of[t]
        here = count > t
        ahead = jnp.clip(count - CUTS[c], 0.0, float(t - CUTS[c]))
        pos = dot(ahead, same) + dot(jnp.where(here, 1.0, 0.0), before) + firsts[c]
        pos_ref[t] = jnp.where(here, pos, -1.0)
        order = run[c] + ahead
        goal_ref[t] = jnp.where(here, within * SECOND[c] + order + 1.0, 0.0)
        column = jnp.sum(jnp.where((i1 == me) & here, order + seconds[c] + 1.0, 0.0), axis=1, keepdims=True) - 1.0
        placed = placed + jnp.where(lane_f == column, slot_col * tiles + (t + 1.0), 0.0)
    place_ref[...] = jnp.sum(placed.reshape(lanes // planes, planes, lanes), axis=1).astype(jnp.int32) - 1
    down = lax.broadcasted_iota(jnp.int32, (total, lanes), 0).astype(f32)
    across = lax.broadcasted_iota(jnp.int32, (total, lanes), 1)
    own = own_ref[...].astype(f32)
    my_row = spot * planes + depth
    block_sum = jnp.zeros((total, lanes), f32)
    tile_sum = jnp.zeros((total, lanes), f32)
    for t in range(tiles):
        hit = pos_ref[t, pl.ds(my_row, 1), :] == down
        block_sum = block_sum + jnp.where(hit, own + 1.0, 0.0)
        tile_sum = tile_sum + jnp.where(hit, float(t), 0.0)
    gather = one(i0 // PLANE == i1)
    pack_ref[...] = ((dot(block_sum, gather) - 1.0) * tiles + dot(tile_sum, gather)).astype(jnp.int32)
    relay = jnp.zeros((total, lanes), f32)
    my_class = lane // PLANE == depth
    for z in range(planes):
        row = spot * planes + z
        got = jnp.zeros((total, lanes), f32)
        for t in range(tiles):
            hit = (pos_ref[t, pl.ds(row, 1), :] == down) & my_class
            got = got + jnp.where(hit, goal_ref[t, pl.ds(row, 1), :], 0.0)
        relay = jnp.where(across == z, jnp.sum(got, axis=1, keepdims=True), relay)
    relay_ref[...] = relay.astype(jnp.int32) - 1


def make_plan(where, table, own):
    lanes = table.shape[1]
    total = sum(FIRST)
    return pl.pallas_call(
        plan_kernel,
        in_specs=[pl.BlockSpec(memory_space=pltpu.SMEM), pl.BlockSpec(memory_space=pltpu.VMEM), pl.BlockSpec(memory_space=pltpu.VMEM)],
        out_specs=[pl.BlockSpec(memory_space=pltpu.SMEM)] + [pl.BlockSpec(memory_space=pltpu.VMEM)] * 3,
        out_shape=[
            jax.ShapeDtypeStruct((1,), jnp.int32),
            jax.ShapeDtypeStruct((total, lanes), jnp.int32),
            jax.ShapeDtypeStruct((total, lanes), jnp.int32),
            jax.ShapeDtypeStruct((PLANE, lanes), jnp.int32),
        ],
        scratch_shapes=[
            pltpu.VMEM((8, lanes, lanes), jnp.float32),
            pltpu.VMEM((8, lanes, lanes), jnp.float32),
        ],
        name="plan",
    )(where, table, own)


def finish(copy, started):
    lax.fori_loop(0, started, lambda _, carry: (copy.wait(), carry)[1], 0)


def pack_kernel(where_ref, pack_ref, mine_ref, theirs_ref, *rest, first, planes):
    outs, done = rest[:-1], rest[-1]
    depth, level = where_ref[1], where_ref[2]
    half_tiles = mine_ref.shape[0]
    size = outs[0].shape[0]
    started = jnp.int32(0)
    for k in range(planes):
        goal = lax.rem(depth + k, planes)

        def body(p, started, k=k, goal=goal):
            item = pack_ref[first + p, goal]
            near = item - level * half_tiles
            far = item - (1 - level) * half_tiles

            @pl.when((item >= 0) & (near >= 0) & (near < half_tiles))
            def _():
                pltpu.make_async_copy(mine_ref.at[near], outs[k].at[p], done).start()

            @pl.when((item >= 0) & (far >= 0) & (far < half_tiles))
            def _():
                pltpu.make_async_copy(theirs_ref.at[far], outs[k].at[p], done).start()

            return started + jnp.where(item >= 0, 1, 0)

        started = lax.fori_loop(0, size, body, started)
    finish(pltpu.make_async_copy(mine_ref.at[0], outs[0].at[0], done), started)


def relay_kernel(where_ref, relay_ref, *rest, first, planes):
    ins, out_ref, done = rest[:planes], rest[planes], rest[planes + 1]
    depth = where_ref[1]
    size = ins[0].shape[0]
    started = jnp.int32(0)
    for k in range(planes):
        source = lax.rem(depth + planes - k, planes)

        def body(p, started, k=k, source=source):
            item = relay_ref[first + p, source]

            @pl.when(item >= 0)
            def _():
                pltpu.make_async_copy(ins[k].at[p], out_ref.at[item], done).start()

            return started + jnp.where(item >= 0, 1, 0)

        started = lax.fori_loop(0, size, body, started)
    finish(pltpu.make_async_copy(ins[0].at[0], out_ref.at[0], done), started)


def place_kernel(place_ref, got_ref, _, out_ref, done, *, first, size):
    def outer(s, started):
        def body(q, started):
            item = place_ref[s, first + q]

            @pl.when(item >= 0)
            def _():
                pltpu.make_async_copy(got_ref.at[s * size + q], out_ref.at[item], done).start()

            return started + jnp.where(item >= 0, 1, 0)

        return lax.fori_loop(0, size, body, started)

    started = lax.fori_loop(0, PLANE, outer, jnp.int32(0))
    finish(pltpu.make_async_copy(got_ref.at[0], out_ref.at[0], done), started)


smem = pl.BlockSpec(memory_space=pltpu.SMEM)
anywhere = pl.BlockSpec(memory_space=pl.ANY)
vmem = pl.BlockSpec(memory_space=pltpu.VMEM)


def two_hops(where, pack, relay, place, mine, theirs, slot_count, block_rows, plane_groups, region_count):
    half = mine.shape[1]
    planes = region_count // PLANE
    tile = lambda n: jax.ShapeDtypeStruct((n, TILE, half), jnp.bfloat16)
    mine, theirs = mine.reshape(-1, TILE, half), theirs.reshape(-1, TILE, half)
    firsts, seconds = starts(FIRST), starts(SECOND)
    arrived = []
    for c, size in enumerate(FIRST):
        sent = pl.pallas_call(
            functools.partial(pack_kernel, first=firsts[c], planes=planes),
            in_specs=[smem, smem, vmem, vmem],
            out_specs=[anywhere] * planes,
            out_shape=[tile(size)] * planes,
            scratch_shapes=[pltpu.SemaphoreType.DMA(())],
            name="pack",
        )(where, pack, mine, theirs)
        where, _ = lax.optimization_barrier((where, sent[0]))
        came = [sent[0]]
        for k in range(1, planes):
            came.append(
                lax.ppermute(sent[k], "region", [(i, (i + k * PLANE) % region_count) for i in range(region_count)])
            )
        arrived.append(came)
    out = jnp.zeros((slot_count * block_rows // TILE, TILE, half), jnp.bfloat16)
    for c, size in enumerate(FIRST):
        onward = pl.pallas_call(
            functools.partial(relay_kernel, first=firsts[c], planes=planes),
            in_specs=[smem, smem] + [vmem] * planes,
            out_specs=anywhere,
            out_shape=tile(PLANE * SECOND[c]),
            scratch_shapes=[pltpu.SemaphoreType.DMA(())],
            name="relay",
        )(where, relay, *arrived[c])
        where, _ = lax.optimization_barrier((where, onward))
        got = lax.all_to_all(
            onward.reshape(PLANE, SECOND[c], TILE, half), "region", 0, 0, axis_index_groups=plane_groups, tiled=True
        ).reshape(-1, TILE, half)
        out = pl.pallas_call(
            functools.partial(place_kernel, first=seconds[c], size=SECOND[c]),
            in_specs=[smem, vmem, anywhere],
            out_specs=anywhere,
            out_shape=jax.ShapeDtypeStruct(out.shape, out.dtype),
            input_output_aliases={2: 0},
            scratch_shapes=[pltpu.SemaphoreType.DMA(())],
            name="place",
        )(place, got, out)
    return out.reshape(slot_count * block_rows, half)


def one_hop(table, new_owner, level, me, mine, theirs, slot_count, block_rows, old_blocks):
    region_count = table.shape[1]
    half = mine.shape[1]
    planes = region_count // PLANE
    first = jnp.where(level == 0, mine, theirs)
    last = jnp.where(level == 0, theirs, mine)
    finished = jnp.concatenate([first, last]).reshape(old_blocks, block_rows, half)
    send = jnp.zeros((region_count, block_rows, half), jnp.bfloat16).at[new_owner].set(finished)
    got = lax.all_to_all(send, "region", 0, 0, tiled=True)
    mine_col = lax.dynamic_index_in_dim(table, me, 1, keepdims=False)
    mine_col = mine_col.reshape(PLANE, planes).T.reshape(-1)
    slots = jnp.where(mine_col > 0, mine_col >> 4, slot_count)
    arrived = jnp.zeros((slot_count, block_rows, half), jnp.bfloat16).at[slots].set(got, mode="drop")
    return arrived.reshape(slot_count * block_rows, half)


def update_and_move(latent, new_owner, dest_slot, live_rows, norm_gain, w_in, b_in, w_out, b_out):
    region_count = lax.axis_size("region")
    planes = region_count // PLANE
    old_blocks = new_owner.shape[0]
    block_rows = latent.shape[0] // old_blocks
    slot_count = old_blocks + old_blocks // 2
    me = lax.axis_index("region")
    level = lax.axis_index("level")
    spot, depth = me % PLANE, me // PLANE
    where = jnp.stack([spot, depth, level]).astype(jnp.int32)
    depth_groups = [[z * PLANE + p for z in range(planes)] for p in range(PLANE)]
    plane_groups = [[z * PLANE + p for p in range(PLANE)] for z in range(planes)]

    tiles = (live_rows + (TILE - 1)) // TILE
    named = new_owner[:, None] == jnp.arange(region_count, dtype=jnp.int32)[None, :]
    entry = jnp.sum(jnp.where(named, (tiles + 16 * dest_slot)[:, None], 0), axis=0)
    own = jnp.sum(jnp.where(named, jnp.arange(old_blocks, dtype=jnp.int32)[:, None], 0), axis=0)
    spread = jnp.broadcast_to(entry[None], (planes, region_count))
    spread = lax.all_to_all(spread, "region", 0, 0, axis_index_groups=depth_groups, tiled=True)
    spread = jnp.broadcast_to(spread[None], (PLANE, planes, region_count))
    table = lax.all_to_all(spread, "region", 0, 0, axis_index_groups=plane_groups, tiled=True)
    table = table.reshape(region_count, region_count)
    fits, pack, relay, place = make_plan(where, table, own[None])

    mine, theirs = node_update(
        latent, live_rows, norm_gain, w_in, b_in, w_out, b_out, old_blocks, block_rows
    )
    return lax.cond(
        fits[0] > 0,
        lambda: two_hops(where, pack, relay, place, mine, theirs, slot_count, block_rows, plane_groups, region_count),
        lambda: one_hop(table, new_owner, level, me, mine, theirs, slot_count, block_rows, old_blocks),
    )


def solution(mesh):
    placed = (
        P("region", "level"),
        P("region"),
        P("region"),
        P("region"),
        P("level"),
        P(),
        P(),
        P(None, "level"),
        P("level"),
    )
    return jax.shard_map(update_and_move, mesh=mesh, in_specs=placed, out_specs=P("region", "level"), check_vma=False)
```

time: 310 us -> 245 us (0.79)
  waiting for transfers between devices: 192 us -> 89.2 us
  starting transfers between devices: 27.8 us -> 85.9 us
  Pallas kernels: 0 us -> 54.5 us
  local copies, waits for them, and re-layouts: 42.1 us -> 10.1 us
  other arithmetic: 14.7 us -> 1.27 us
  between operations: 13.5 us -> 0.92 us
  matrix products: 11.6 us -> 0 us
  blocking collectives: 6.66 us -> 0 us
    all_to_all x2 -> x5, waiting for transfers between devices: 185 us -> 21.6 us  [the longest x3 9.26 us: two_hops(): lax.all_to_all(onward.reshape(PLANE, SECOND[c], TILE, half), 'region', 0,...]
    ppermute x0 -> x25, waiting for transfers between devices: none -> 67.5 us  [the longest x21 62.1 us: two_hops(): lax.ppermute(sent[k], 'region', [(i, (i + k * PLANE) % region_count) for...]
    pallas_call x0 -> x11, Pallas kernels: none -> 54.5 us  [the longest x1 14.3 us: node_update(): mlp(level[None], live, latent, theirs, sides, side_theirs, w_in, b_in[Non...]
    ppermute x0 -> x25, starting transfers between devices: none -> 53.7 us  [the longest x21 49.4 us: two_hops(): lax.ppermute(sent[k], 'region', [(i, (i + k * PLANE) % region_count) for...]
    scatter x3 -> x0, local copies, waits for them, and re-layouts: 34.1 us -> none  [the longest x1 21.4 us: shards(): arrived = jnp.zeros((slot_count, block_rows, half_width), jnp.bfloat16).a...]
    dot_general x1 -> x0, matrix products: 11.6 us -> none  [node_update(): jnp.dot(hidden, w_out, preferred_element_type=jnp.float32) + b_out + inputs]
    all_gather x1 -> x0, waiting for transfers between devices: 7.55 us -> none  [node_update(): normed = lax.all_gather(half_normed, 'level', axis=1, tiled=True)]
    convert_element_type x1 -> x0, other arithmetic: 7.06 us -> none  [node_update(): half_normed = ((inputs - average[:, None]) * lax.rsqrt(variance + epsilon...]
  transfers between devices with their start and end apart: 3 -> 30, of which waited for: 2 -> 16; matrix products, arithmetic and copies ran while one was open for 10% -> 2% of each run, Pallas kernels for 0% -> 11%
where the time goes in v1:
time: 245 us; the launch traced here: 242 us
  waiting for transfers between devices  89.2 us (36%)
  starting transfers between devices  85.9 us (35%)
  Pallas kernels  54.5 us (22%)
  local copies, waits for them, and re-layouts  10.1 us (4%)
    ppermute x21, waiting for transfers between devices, two_hops(): lax.ppermute(sent[k], 'region', [(i, (i + k * PLANE) % region_count) for...  62.1 us
    ppermute x21, starting transfers between devices, two_hops(): lax.ppermute(sent[k], 'region', [(i, (i + k * PLANE) % region_count) for...  49.4 us
    all_to_all x3, starting transfers between devices, two_hops(): lax.all_to_all(onward.reshape(PLANE, SECOND[c], TILE, half), 'region', 0,...  19 us
    pallas_call x1, Pallas kernels, node_update(): mlp(level[None], live, latent, theirs, sides, side_theirs, w_in, b_in[Non...  14.3 us
    pallas_call x3, Pallas kernels, two_hops(): pl.pallas_call(functools.partial(place_kernel, first=seconds[c], size=SEC...  13.5 us
    pallas_call x3, Pallas kernels, two_hops(): pl.pallas_call(functools.partial(pack_kernel, first=firsts[c], planes=pla...  13.3 us
    pallas_call x3, Pallas kernels, two_hops(): pl.pallas_call(functools.partial(relay_kernel, first=firsts[c], planes=pl...  11.5 us
    all_to_all x3, waiting for transfers between devices, two_hops(): lax.all_to_all(onward.reshape(PLANE, SECOND[c], TILE, half), 'region', 0,...  9.26 us
  transfers between devices with their start and end apart: 30, of which 16 were waited for; matrix products, arithmetic and copies ran while one was open for 2% of the time, Pallas kernels for 11%

profile of v1, /device:TPU:1, one launch (start us, length us, event | category | flops | bytes accessed | tf_op | source)
XLA Modules:
  0.0 242.5 jit_solution(918022297417782687)
XLA Ops:
  0.0 2.2 constant_dynamic-slice_fusion
  2.2 3.3 %collective-permute-start.21 = (f32[3328,256]{1,0:T(8,128)S(1)}, f32[3328,256]{1,0:T(8,128)S(1)}, u32[]{:S(2)}, u32[]{:S(2)}) collective-permute-start(f32[3328,256]{1,0:T(8,128)S(1)} %constant_dynamic-slice_fusion), channel_id=1, source_target_pairs={{0,1},{1,0},{2,3},{3,2},{4,5},{5,4},{6,7},{7,6},{8,9},{9,8},{10,11... | collective-permute-start | bytes 10223624 | tf_op jit(solution)/shard_map/ppermute | solution.py:68
  6.1 5.4 %collective-permute-done.22.side_theirs_ref = f32[2,256]{1,0:T(2,128)S(1)} collective-permute-done((f32[2,256]{1,0:T(2,128)S(1)}, f32[2,256]{1,0:T(2,128)S(1)}, u32[]{:S(2)}, u32[]{:S(2)}) %collective-permute-start.22) | collective-permute-done | bytes 2080 | tf_op jit(solution)/shard_map/ppermute | solution.py:70
  13.4 14.3 %node_mlp.1 = (bf16[3328,256]{1,0:T(8,128)(2,1)S(1)}, bf16[3328,256]{1,0:T(8,128)(2,1)}) custom-call(s32[1]{0:T(128)} %bitcast.15.level_ref, s32[52]{0:T(128)} %live_ref.1, f32[6656,256]{1,0:T(8,128)} %mine_ref.1, f32[3328,256]{1,0:T(8,128)} %copy-done.1, f32[2,256]{1,0:T(2,128)} %copy-done.19, f32[2,256]{1,0:T(2,128)} %copy-done.20, ...), custom_call_target="tpu_custom_call" | custom-call | tf_op jit(solution)/shard_map/node_mlp/pallas_call | solution.py:98
  29.3 6.5 %all-to-all-start.4 = ((s32[8,1,128]{2,1,0:T(1,128)}), s32[8,1,128]{2,1,0:T(1,128)S(1)}, u32[]{:S(2)}, u32[]{:S(2)}) async-start(s32[8,1,128]{2,1,0:T(1,128)} %broadcast_in_dim.53), calls=%async_computation.4 | async-start | bytes 8192 | tf_op jit(solution)/shard_map/all_to_all | solution.py:351
  35.8 6.5 %all-to-all-done.4 = s32[8,1,128]{2,1,0:T(1,128)S(1)} async-done(((s32[8,1,128]{2,1,0:T(1,128)}), s32[8,1,128]{2,1,0:T(1,128)S(1)}, u32[]{:S(2)}, u32[]{:S(2)}) %all-to-all-start.4) | async-done | bytes 4128 | tf_op jit(solution)/shard_map/all_to_all | solution.py:351
  42.9 6.8 %all-to-all-start.5 = ((s32[16,8,128]{2,1,0:T(8,128)}), s32[16,8,128]{2,1,0:T(8,128)S(1)}, u32[]{:S(2)}, u32[]{:S(2)}) async-start(s32[16,8,128]{2,1,0:T(8,128)} %broadcast_in_dim.55), calls=%async_computation.5 | async-start | bytes 131072 | tf_op jit(solution)/shard_map/all_to_all | solution.py:353
  50.3 5.9 %all-to-all-done.5 = s32[16,8,128]{2,1,0:T(8,128)S(1)} async-done(((s32[16,8,128]{2,1,0:T(8,128)}), s32[16,8,128]{2,1,0:T(8,128)S(1)}, u32[]{:S(2)}, u32[]{:S(2)}) %all-to-all-start.5) | async-done | bytes 65568 | tf_op jit(solution)/shard_map/all_to_all | solution.py:353
  56.2 1.9 plan.1
  58.8 183.5 %conditional.1 = (bf16[9984,256]{1,0:T(8,128)(2,1)}) conditional(s32[]{:T(128)} %bitcast.19, (s32[]{:T(128)}, s32[128,128]{1,0:T(8,128)S(1)}, s32[52]{0:T(128)}, s32[]{:T(128)}, bf16[3328,256]{1,0:T(8,128)(2,1)S(1)}, /*index=5*/bf16[3328,256]{1,0:T(8,128)(2,1)S(1)}) %tuple.28, (bf16[3328,256]{1,0:T(8,128)(2,1)S(1)}, bf16[3328,256]{1,0:T(8,128)(2,1)S(1)}, ...), branch_computations={%region_2.5_spmd, %region_5.6_spmd} | conditional | flops 8520608 | bytes 87824584 | solution.py:360
  58.8 5.2 %pack.3 = (bf16[27,16,256]{2,1,0:T(8,128)(2,1)}, bf16[27,16,256]{2,1,0:T(8,128)(2,1)}, bf16[27,16,256]{2,1,0:T(8,128)(2,1)}, bf16[27,16,256]{2,1,0:T(8,128)(2,1)...) custom-call(s32[3]{0:T(128)} %get-tuple-element.65.where_ref, ...), custom_call_target="tpu_custom_call" | custom-call | tf_op jit(solution)/shard_map/cond/branch_1_fun/pack/pallas_call | solution.py:276
  64.6 2.1 collective-permute-start.2
  66.7 3.3 %collective-permute-start.3 = (bf16[27,16,256]{2,1,0:T(8,128)(2,1)}, bf16[27,16,256]{2,1,0:T(8,128)(2,1)}, u32[]{:S(2)}, u32[]{:S(2)}) collective-permute-start(bf16[27,16,256]{2,1,0:T(8,128)(2,1)} %get-tuple-element.53), channel_id=1, source_target_pairs={{0,128},{2,130},{4,132},{6,134},{8,136},{10,138},{12,140},{14,142}... | collective-permute-start | bytes 663560 | tf_op jit(solution)/shard_map/cond/branch_1_fun/ppermute | solution.py:288
  70.1 2.1 collective-permute-start.4
  74.6 3.5 %collective-permute-start.6 = (bf16[27,16,256]{2,1,0:T(8,128)(2,1)}, bf16[27,16,256]{2,1,0:T(8,128)(2,1)}, u32[]{:S(2)}, u32[]{:S(2)}) collective-permute-start(bf16[27,16,256]{2,1,0:T(8,128)(2,1)} %get-tuple-element.56), channel_id=1, source_target_pairs={{0,224},{2,226},{4,228},{6,230},{8,232},{10,234},{12,236},{14,238}... | collective-permute-start | bytes 663560 | tf_op jit(solution)/shard_map/cond/branch_1_fun/ppermute | solution.py:288
  78.1 4.6 %pack.4 = (bf16[25,16,256]{2,1,0:T(8,128)(2,1)}, bf16[25,16,256]{2,1,0:T(8,128)(2,1)}, bf16[25,16,256]{2,1,0:T(8,128)(2,1)}, bf16[25,16,256]{2,1,0:T(8,128)(2,1)...) custom-call(s32[3]{0:T(128)S(1)} %copy-done.18, ...), custom_call_target="tpu_custom_call" | custom-call | tf_op jit(solution)/shard_map/cond/branch_1_fun/pack/pallas_call | solution.py:276
  82.7 3.4 %pack.5 = (bf16[15,16,256]{2,1,0:T(8,128)(2,1)}, bf16[15,16,256]{2,1,0:T(8,128)(2,1)}, bf16[15,16,256]{2,1,0:T(8,128)(2,1)}, bf16[15,16,256]{2,1,0:T(8,128)(2,1)...) custom-call(s32[3]{0:T(128)S(1)} %copy-done.18, ...), custom_call_target="tpu_custom_call" | custom-call | tf_op jit(solution)/shard_map/cond/branch_1_fun/pack/pallas_call | solution.py:276
  86.2 2.9 %collective-permute-done.2.rest_3_ = bf16[27,16,256]{2,1,0:T(8,128)(2,1)} collective-permute-done((bf16[27,16,256]{2,1,0:T(8,128)(2,1)}, bf16[27,16,256]{2,1,0:T(8,128)(2,1)}, u32[]{:S(2)}, u32[]{:S(2)}) %collective-permute-start.2) | collective-permute-done | bytes 221216 | tf_op jit(solution)/shard_map/cond/branch_1_fun/ppermute | solution.py:288
  89.0 5.4 %collective-permute-done.3.rest_4_ = bf16[27,16,256]{2,1,0:T(8,128)(2,1)} collective-permute-done((bf16[27,16,256]{2,1,0:T(8,128)(2,1)}, bf16[27,16,256]{2,1,0:T(8,128)(2,1)}, u32[]{:S(2)}, u32[]{:S(2)}) %collective-permute-start.3) | collective-permute-done | bytes 221216 | tf_op jit(solution)/shard_map/cond/branch_1_fun/ppermute | solution.py:288
  94.5 9.6 %collective-permute-done.5.rest_6_ = bf16[27,16,256]{2,1,0:T(8,128)(2,1)} collective-permute-done((bf16[27,16,256]{2,1,0:T(8,128)(2,1)}, bf16[27,16,256]{2,1,0:T(8,128)(2,1)}, u32[]{:S(2)}, u32[]{:S(2)}) %collective-permute-start.5) | collective-permute-done | bytes 221216 | tf_op jit(solution)/shard_map/cond/branch_1_fun/ppermute | solution.py:288
  104.1 4.6 %collective-permute-done.6.rest_7_ = bf16[27,16,256]{2,1,0:T(8,128)(2,1)} collective-permute-done((bf16[27,16,256]{2,1,0:T(8,128)(2,1)}, bf16[27,16,256]{2,1,0:T(8,128)(2,1)}, u32[]{:S(2)}, u32[]{:S(2)}) %collective-permute-start.6) | collective-permute-done | bytes 221216 | tf_op jit(solution)/shard_map/cond/branch_1_fun/ppermute | solution.py:288
  108.7 4.6 %relay.3 = bf16[240,16,256]{2,1,0:T(8,128)(2,1)} custom-call(s32[3]{0:T(128)S(1)} %copy-done.18, s32[67,128]{1,0:T(8,128)S(1)} %get-tuple-element.49.relay_ref, bf16[27,16,256]{2,1,0:T(8,128)(2,1)} %get-tuple-element.43.rest_0_, bf16[27,16,256]{2,1,0:T(8,128)(2,1)} %collective-permute-done.rest_1_, bf16[27,16,256]{2,1,0:T(8,128)(2,1)} %collective-permute-done.1.rest_2_, ...), custom_call_target="tpu_custom_call" | custom-call | tf_op jit(solution)/shard_map/cond/branch_1_fun/relay/pallas_call | solution.py:293
  113.3 3.7 %all-to-all-start.2 = ((bf16[16,15,16,256]{3,2,1,0:T(8,128)(2,1)}), bf16[16,15,16,256]{3,2,1,0:T(8,128)(2,1)S(1)}, u32[]{:S(2)}, u32[]{:S(2)}) async-start(bf16[16,15,16,256]{3,2,1,0:T(8,128)(2,1)} %bitcast.33), calls=%async_computation.2 | async-start | bytes 3932160 | tf_op jit(solution)/shard_map/cond/branch_1_fun/all_to_all | solution.py:302
  117.0 2.9 %collective-permute-start.10 = (bf16[25,16,256]{2,1,0:T(8,128)(2,1)S(1)}, bf16[25,16,256]{2,1,0:T(8,128)(2,1)S(1)}, u32[]{:S(2)}, u32[]{:S(2)}) collective-permute-start(bf16[25,16,256]{2,1,0:T(8,128)(2,1)S(1)} %copy-done.26), channel_id=1, source_target_pairs={{0,128},{2,130},{4,132},{6,134},{8,136},{10,138},{12,140},{14,142}... | collective-permute-start | bytes 614408 | tf_op jit(solution)/shard_map/cond/branch_1_fun/ppermute | solution.py:288
  120.0 2.5 %collective-permute-start.11 = (bf16[25,16,256]{2,1,0:T(8,128)(2,1)S(1)}, bf16[25,16,256]{2,1,0:T(8,128)(2,1)S(1)}, u32[]{:S(2)}, u32[]{:S(2)}) collective-permute-start(bf16[25,16,256]{2,1,0:T(8,128)(2,1)S(1)} %copy-done.25), channel_id=1, source_target_pairs={{0,160},{2,162},{4,164},{6,166},{8,168},{10,170},{12,172},{14,174}... | collective-permute-start | bytes 614408 | tf_op jit(solution)/shard_map/cond/branch_1_fun/ppermute | solution.py:288
  122.5 3.3 %collective-permute-start.12 = (bf16[25,16,256]{2,1,0:T(8,128)(2,1)}, bf16[25,16,256]{2,1,0:T(8,128)(2,1)S(1)}, u32[]{:S(2)}, u32[]{:S(2)}) collective-permute-start(bf16[25,16,256]{2,1,0:T(8,128)(2,1)} %get-tuple-element.63), channel_id=1, source_target_pairs={{0,192},{2,194},{4,196},{6,198},{8,200},{10,202},{12,204},{14,206}... | collective-permute-start | bytes 614408 | tf_op jit(solution)/shard_map/cond/branch_1_fun/ppermute | solution.py:288
  127.3 2.8 %collective-permute-start.8 = (bf16[25,16,256]{2,1,0:T(8,128)(2,1)}, bf16[25,16,256]{2,1,0:T(8,128)(2,1)S(1)}, u32[]{:S(2)}, u32[]{:S(2)}) collective-permute-start(bf16[25,16,256]{2,1,0:T(8,128)(2,1)} %get-tuple-element.59), channel_id=1, source_target_pairs={{0,64},{2,66},{4,68},{6,70},{8,72},{10,74},{12,76},{14,78},{16,80}... | collective-permute-start | bytes 614408 | tf_op jit(solution)/shard_map/cond/branch_1_fun/ppermute | solution.py:288
  130.0 15.2 %collective-permute-done.11.rest_5_ = bf16[25,16,256]{2,1,0:T(8,128)(2,1)S(1)} collective-permute-done((bf16[25,16,256]{2,1,0:T(8,128)(2,1)S(1)}, bf16[25,16,256]{2,1,0:T(8,128)(2,1)S(1)}, u32[]{:S(2)}, u32[]{:S(2)}) %collective-permute-start.11) | collective-permute-done | bytes 204832 | tf_op jit(solution)/shard_map/cond/branch_1_fun/ppermute | solution.py:288
  145.2 5.1 %collective-permute-start.9 = (bf16[25,16,256]{2,1,0:T(8,128)(2,1)}, bf16[25,16,256]{2,1,0:T(8,128)(2,1)S(1)}, u32[]{:S(2)}, u32[]{:S(2)}) collective-permute-start(bf16[25,16,256]{2,1,0:T(8,128)(2,1)} %get-tuple-element.60), channel_id=1, source_target_pairs={{0,96},{2,98},{4,100},{6,102},{8,104},{10,106},{12,108},{14,110},{... | collective-permute-start | bytes 614408 | tf_op jit(solution)/shard_map/cond/branch_1_fun/ppermute | solution.py:288
  150.4 4.9 %collective-permute-done.12.rest_6_ = bf16[25,16,256]{2,1,0:T(8,128)(2,1)S(1)} collective-permute-done((bf16[25,16,256]{2,1,0:T(8,128)(2,1)}, bf16[25,16,256]{2,1,0:T(8,128)(2,1)S(1)}, u32[]{:S(2)}, u32[]{:S(2)}) %collective-permute-start.12) | collective-permute-done | bytes 204832 | tf_op jit(solution)/shard_map/cond/branch_1_fun/ppermute | solution.py:288
  155.2 3.6 %collective-permute-done.13.rest_7_ = bf16[25,16,256]{2,1,0:T(8,128)(2,1)S(1)} collective-permute-done((bf16[25,16,256]{2,1,0:T(8,128)(2,1)}, bf16[25,16,256]{2,1,0:T(8,128)(2,1)S(1)}, u32[]{:S(2)}, u32[]{:S(2)}) %collective-permute-start.13) | collective-permute-done | bytes 204832 | tf_op jit(solution)/shard_map/cond/branch_1_fun/ppermute | solution.py:288
  160.3 4.0 %relay.4 = bf16[240,16,256]{2,1,0:T(8,128)(2,1)} custom-call(s32[3]{0:T(128)S(1)} %copy-done.18, s32[67,128]{1,0:T(8,128)S(1)} %get-tuple-element.49.relay_ref, bf16[25,16,256]{2,1,0:T(8,128)(2,1)} %get-tuple-element.45.rest_0_, bf16[25,16,256]{2,1,0:T(8,128)(2,1)} %copy-done.8, bf16[25,16,256]{2,1,0:T(8,128)(2,1)} %copy-done.9, ...), custom_call_target="tpu_custom_call" | custom-call | tf_op jit(solution)/shard_map/cond/branch_1_fun/relay/pallas_call | solution.py:293
  164.4 9.0 %all-to-all-start.1 = ((bf16[16,15,16,256]{3,2,1,0:T(8,128)(2,1)}), bf16[16,15,16,256]{3,2,1,0:T(8,128)(2,1)}, u32[]{:S(2)}, u32[]{:S(2)}) async-start(bf16[16,15,16,256]{3,2,1,0:T(8,128)(2,1)} %bitcast.35), calls=%async_computation.1 | async-start | bytes 3932160 | tf_op jit(solution)/shard_map/cond/branch_1_fun/all_to_all | solution.py:302
  173.3 2.2 collective-permute-start.14
  175.6 3.8 %collective-permute-start.15 = (bf16[15,16,256]{2,1,0:T(8,128)(2,1)S(1)}, bf16[15,16,256]{2,1,0:T(8,128)(2,1)S(1)}, u32[]{:S(2)}, u32[]{:S(2)}) collective-permute-start(bf16[15,16,256]{2,1,0:T(8,128)(2,1)S(1)} %copy-done.31), channel_id=1, source_target_pairs={{0,64},{2,66},{4,68},{6,70},{8,72},{10,74},{12,76},{14,78},{16,80}... | collective-permute-start | bytes 368648 | tf_op jit(solution)/shard_map/cond/branch_1_fun/ppermute | solution.py:288
  179.3 1.9 collective-permute-start.16
  182.8 2.7 %collective-permute-start.18 = (bf16[15,16,256]{2,1,0:T(8,128)(2,1)S(1)}, bf16[15,16,256]{2,1,0:T(8,128)(2,1)S(1)}, u32[]{:S(2)}, u32[]{:S(2)}) collective-permute-start(bf16[15,16,256]{2,1,0:T(8,128)(2,1)S(1)} %copy-done.29), channel_id=1, source_target_pairs={{0,160},{2,162},{4,164},{6,166},{8,168},{10,170},{12,172},{14,174}... | collective-permute-start | bytes 368648 | tf_op jit(solution)/shard_map/cond/branch_1_fun/ppermute | solution.py:288
  187.2 4.8 %collective-permute-start.20 = (bf16[15,16,256]{2,1,0:T(8,128)(2,1)S(1)}, bf16[15,16,256]{2,1,0:T(8,128)(2,1)S(1)}, u32[]{:S(2)}, u32[]{:S(2)}) collective-permute-start(bf16[15,16,256]{2,1,0:T(8,128)(2,1)S(1)} %copy-done.27), channel_id=1, source_target_pairs={{0,224},{2,226},{4,228},{6,230},{8,232},{10,234},{12,236},{14,238}... | collective-permute-start | bytes 368648 | tf_op jit(solution)/shard_map/cond/branch_1_fun/ppermute | solution.py:288
  192.0 7.1 %collective-permute-done.16.rest_3_ = bf16[15,16,256]{2,1,0:T(8,128)(2,1)S(1)} collective-permute-done((bf16[15,16,256]{2,1,0:T(8,128)(2,1)}, bf16[15,16,256]{2,1,0:T(8,128)(2,1)S(1)}, u32[]{:S(2)}, u32[]{:S(2)}) %collective-permute-start.16) | collective-permute-done | bytes 122912 | tf_op jit(solution)/shard_map/cond/branch_1_fun/ppermute | solution.py:288
  199.1 5.0 %collective-permute-done.19.rest_6_ = bf16[15,16,256]{2,1,0:T(8,128)(2,1)S(1)} collective-permute-done((bf16[15,16,256]{2,1,0:T(8,128)(2,1)S(1)}, bf16[15,16,256]{2,1,0:T(8,128)(2,1)S(1)}, u32[]{:S(2)}, u32[]{:S(2)}) %collective-permute-start.19) | collective-permute-done | bytes 122912 | tf_op jit(solution)/shard_map/cond/branch_1_fun/ppermute | solution.py:288
  204.1 2.6 %collective-permute-done.20.rest_7_ = bf16[15,16,256]{2,1,0:T(8,128)(2,1)S(1)} collective-permute-done((bf16[15,16,256]{2,1,0:T(8,128)(2,1)S(1)}, bf16[15,16,256]{2,1,0:T(8,128)(2,1)S(1)}, u32[]{:S(2)}, u32[]{:S(2)}) %collective-permute-start.20) | collective-permute-done | bytes 122912 | tf_op jit(solution)/shard_map/cond/branch_1_fun/ppermute | solution.py:288
  207.3 3.0 %relay.5 = bf16[192,16,256]{2,1,0:T(8,128)(2,1)} custom-call(s32[3]{0:T(128)S(1)} %copy-done.18, s32[67,128]{1,0:T(8,128)S(1)} %get-tuple-element.49.relay_ref, bf16[15,16,256]{2,1,0:T(8,128)(2,1)} %get-tuple-element.47.rest_0_, bf16[15,16,256]{2,1,0:T(8,128)(2,1)} %copy-done.11, bf16[15,16,256]{2,1,0:T(8,128)(2,1)} %copy-done.12, ...), custom_call_target="tpu_custom_call" | custom-call | tf_op jit(solution)/shard_map/cond/branch_1_fun/relay/pallas_call | solution.py:293
  210.3 6.3 %all-to-all-start = ((bf16[16,12,16,256]{3,2,1,0:T(8,128)(2,1)}), bf16[16,12,16,256]{3,2,1,0:T(8,128)(2,1)}, u32[]{:S(2)}, u32[]{:S(2)}) async-start(bf16[16,12,16,256]{3,2,1,0:T(8,128)(2,1)} %bitcast.36), calls=%async_computation | async-start | bytes 3145728 | tf_op jit(solution)/shard_map/cond/branch_1_fun/all_to_all | solution.py:302
  216.7 2.6 %broadcast_15__.0._ = bf16[624,16,256]{2,1,0:T(8,128)(2,1)} broadcast(bf16[]{:T(256)} %constant.61.clone), dimensions={} | broadcast | bytes 5111810 | tf_op jit(solution)/shard_map/broadcast.15._
  219.3 5.0 %place.3._ = bf16[624,16,256]{2,1,0:T(8,128)(2,1)} custom-call(s32[16,128]{1,0:T(8,128)S(1)} %get-tuple-element.38.place_ref, bf16[240,16,256]{2,1,0:T(8,128)(2,1)} %bitcast.34, bf16[624,16,256]{2,1,0:T(8,128)(2,1)} %broadcast_15__.0._), custom_call_target="tpu_custom_call", output_to_operand_aliasing={{}: (2, {})} | custom-call | tf_op jit(solution)/shard_map/cond/branch_1_fun/place/pallas_call | solution.py:305
  224.3 4.6 %place.4._ = bf16[624,16,256]{2,1,0:T(8,128)(2,1)} custom-call(s32[16,128]{1,0:T(8,128)S(1)} %get-tuple-element.38.place_ref, bf16[240,16,256]{2,1,0:T(8,128)(2,1)} %bitcast.9.got_ref, bf16[624,16,256]{2,1,0:T(8,128)(2,1)} %place.3._), custom_call_target="tpu_custom_call", output_to_operand_aliasing={{}: (2, {})} | custom-call | tf_op jit(solution)/shard_map/cond/branch_1_fun/place/pallas_call | solution.py:305
  228.9 9.3 %all-to-all-done = bf16[16,12,16,256]{3,2,1,0:T(8,128)(2,1)} async-done(((bf16[16,12,16,256]{3,2,1,0:T(8,128)(2,1)}), bf16[16,12,16,256]{3,2,1,0:T(8,128)(2,1)}, u32[]{:S(2)}, u32[]{:S(2)}) %all-to-all-start) | async-done | bytes 1572896 | tf_op jit(solution)/shard_map/cond/branch_1_fun/all_to_all | solution.py:302
  238.2 3.9 %place.5 = bf16[624,16,256]{2,1,0:T(8,128)(2,1)} custom-call(s32[16,128]{1,0:T(8,128)S(1)} %get-tuple-element.38.place_ref, bf16[192,16,256]{2,1,0:T(8,128)(2,1)} %bitcast.7.got_ref, bf16[624,16,256]{2,1,0:T(8,128)(2,1)} %place.4._), custom_call_target="tpu_custom_call", output_to_operand_aliasing={{}: (2, {})} | custom-call | tf_op jit(solution)/shard_map/cond/branch_1_fun/place/pallas_call | solution.py:305
  (100 shorter events, 15.3 us)
Async XLA Ops:
  2.2 9.3 %collective-permute-start.21 = (f32[3328,256]{1,0:T(8,128)S(1)}, f32[3328,256]{1,0:T(8,128)S(1)}, u32[]{:S(2)}, u32[]{:S(2)}) collective-permute-start(f32[3328,256]{1,0:T(8,128)S(1)} %constant_dynamic-slice_fusion), channel_id=1, source_target_pairs={{0,1},{1,0},{2,3},{3,2},{4,5},{5,4},{6,7},{7,6},{8,9},{9,8},{10,11... | collective-permute-start | bytes 10223624 | tf_op jit(solution)/shard_map/ppermute | solution.py:68
  5.5 6.0 %collective-permute-start.23 = (bf16[512,256]{1,0:T(8,128)(2,1)S(1)}, bf16[512,256]{1,0:T(8,128)(2,1)S(1)}, u32[]{:S(2)}, u32[]{:S(2)}) collective-permute-start(bf16[512,256]{1,0:T(8,128)(2,1)S(1)} %copy-done.2), channel_id=1, source_target_pairs={{0,1},{1,0},{2,3},{3,2},{4,5},{5,4},{6,7},{7,6},{8,9},{9,8},{10,11... | collective-permute-start | bytes 786440 | tf_op jit(solution)/shard_map/ppermute | solution.py:69
  5.6 7.8 %copy-start.19 = (f32[2,256]{1,0:T(2,128)}, f32[2,256]{1,0:T(2,128)S(1)}, u32[]{:S(2)}) copy-start(f32[2,256]{1,0:T(2,128)S(1)} %pad_maximum_fusion.1.side_mine_ref) | copy-start | bytes 6148
  5.7 5.9 %collective-permute-start.22 = (f32[2,256]{1,0:T(2,128)S(1)}, f32[2,256]{1,0:T(2,128)S(1)}, u32[]{:S(2)}, u32[]{:S(2)}) collective-permute-start(f32[2,256]{1,0:T(2,128)S(1)} %pad_maximum_fusion.1.side_mine_ref), channel_id=1, source_target_pairs={{0,1},{1,0},{2,3},{3,2},{4,5},{5,4},{6,7},{7,6},{8,9},{9,8},{10,11... | collective-permute-start | bytes 6152 | tf_op jit(solution)/shard_map/ppermute | solution.py:70
  13.4 14.7 %copy-start.23 = (s32[52]{0:T(128)S(1)}, s32[52]{0:T(128)}, u32[]{:S(2)}) copy-start(s32[52]{0:T(128)} %live_ref.1) | copy-start | bytes 628
  13.4 14.7 %copy-start.33 = (s32[52]{0:T(128)S(1)}, s32[52]{0:T(128)}, u32[]{:S(2)}) copy-start(s32[52]{0:T(128)} %param.13) | copy-start | bytes 628
  13.4 14.7 %copy-start.24 = (s32[52]{0:T(128)S(1)}, s32[52]{0:T(128)}, u32[]{:S(2)}) copy-start(s32[52]{0:T(128)} %param.12) | copy-start | bytes 628
  27.7 31.0 %collective-permute-start.24 = (bf16[3328,256]{1,0:T(8,128)(2,1)}, bf16[3328,256]{1,0:T(8,128)(2,1)S(1)}, u32[]{:S(2)}, u32[]{:S(2)}) collective-permute-start(bf16[3328,256]{1,0:T(8,128)(2,1)} %get-tuple-element.81), channel_id=1, source_target_pairs={{0,1},{1,0},{2,3},{3,2},{4,5},{5,4},{6,7},{7,6},{8,9},{9,8},{10,11... | collective-permute-start | bytes 5111816 | tf_op jit(solution)/shard_map/ppermute | solution.py:99
  29.3 13.0 %all-to-all-start.4 = ((s32[8,1,128]{2,1,0:T(1,128)}), s32[8,1,128]{2,1,0:T(1,128)S(1)}, u32[]{:S(2)}, u32[]{:S(2)}) async-start(s32[8,1,128]{2,1,0:T(1,128)} %broadcast_in_dim.53), calls=%async_computation.4 | async-start | bytes 8192 | tf_op jit(solution)/shard_map/all_to_all | solution.py:351
  42.9 13.3 %all-to-all-start.5 = ((s32[16,8,128]{2,1,0:T(8,128)}), s32[16,8,128]{2,1,0:T(8,128)S(1)}, u32[]{:S(2)}, u32[]{:S(2)}) async-start(s32[16,8,128]{2,1,0:T(8,128)} %broadcast_in_dim.55), calls=%async_computation.5 | async-start | bytes 131072 | tf_op jit(solution)/shard_map/all_to_all | solution.py:353
  58.8 19.3 %copy-start.18 = (s32[3]{0:T(128)S(1)}, s32[3]{0:T(128)}, u32[]{:S(2)}) copy-start(s32[3]{0:T(128)} %get-tuple-element.65.where_ref) | copy-start | bytes 40 | tf_op jit(solution)/shard_map/cond
  64.0 8.5 %collective-permute-start = (bf16[27,16,256]{2,1,0:T(8,128)(2,1)}, bf16[27,16,256]{2,1,0:T(8,128)(2,1)}, u32[]{:S(2)}, u32[]{:S(2)}) collective-permute-start(bf16[27,16,256]{2,1,0:T(8,128)(2,1)} %get-tuple-element.50), channel_id=1, source_target_pairs={{0,32},{2,34},{4,36},{6,38},{8,40},{10,42},{12,44},{14,46},{16,48}... | collective-permute-start | bytes 663560 | tf_op jit(solution)/shard_map/cond/branch_1_fun/ppermute | solution.py:288
  64.4 10.2 %collective-permute-start.1 = (bf16[27,16,256]{2,1,0:T(8,128)(2,1)}, bf16[27,16,256]{2,1,0:T(8,128)(2,1)}, u32[]{:S(2)}, u32[]{:S(2)}) collective-permute-start(bf16[27,16,256]{2,1,0:T(8,128)(2,1)} %get-tuple-element.51), channel_id=1, source_target_pairs={{0,64},{2,66},{4,68},{6,70},{8,72},{10,74},{12,76},{14,78},{16,80}... | collective-permute-start | bytes 663560 | tf_op jit(solution)/shard_map/cond/branch_1_fun/ppermute | solution.py:288
  64.6 24.4 %collective-permute-start.2 = (bf16[27,16,256]{2,1,0:T(8,128)(2,1)}, bf16[27,16,256]{2,1,0:T(8,128)(2,1)}, u32[]{:S(2)}, u32[]{:S(2)}) collective-permute-start(bf16[27,16,256]{2,1,0:T(8,128)(2,1)} %get-tuple-element.52), channel_id=1, source_target_pairs={{0,96},{2,98},{4,100},{6,102},{8,104},{10,106},{12,108},{14,110},{... | collective-permute-start | bytes 663560 | tf_op jit(solution)/shard_map/cond/branch_1_fun/ppermute | solution.py:288
  66.7 27.7 %collective-permute-start.3 = (bf16[27,16,256]{2,1,0:T(8,128)(2,1)}, bf16[27,16,256]{2,1,0:T(8,128)(2,1)}, u32[]{:S(2)}, u32[]{:S(2)}) collective-permute-start(bf16[27,16,256]{2,1,0:T(8,128)(2,1)} %get-tuple-element.53), channel_id=1, source_target_pairs={{0,128},{2,130},{4,132},{6,134},{8,136},{10,138},{12,140},{14,142}... | collective-permute-start | bytes 663560 | tf_op jit(solution)/shard_map/cond/branch_1_fun/ppermute | solution.py:288
  70.1 24.4 %collective-permute-start.4 = (bf16[27,16,256]{2,1,0:T(8,128)(2,1)}, bf16[27,16,256]{2,1,0:T(8,128)(2,1)}, u32[]{:S(2)}, u32[]{:S(2)}) collective-permute-start(bf16[27,16,256]{2,1,0:T(8,128)(2,1)} %get-tuple-element.54), channel_id=1, source_target_pairs={{0,160},{2,162},{4,164},{6,166},{8,168},{10,170},{12,172},{14,174}... | collective-permute-start | bytes 663560 | tf_op jit(solution)/shard_map/cond/branch_1_fun/ppermute | solution.py:288
  72.5 31.5 %collective-permute-start.5 = (bf16[27,16,256]{2,1,0:T(8,128)(2,1)}, bf16[27,16,256]{2,1,0:T(8,128)(2,1)}, u32[]{:S(2)}, u32[]{:S(2)}) collective-permute-start(bf16[27,16,256]{2,1,0:T(8,128)(2,1)} %get-tuple-element.55), channel_id=1, source_target_pairs={{0,192},{2,194},{4,196},{6,198},{8,200},{10,202},{12,204},{14,206}... | collective-permute-start | bytes 663560 | tf_op jit(solution)/shard_map/cond/branch_1_fun/ppermute | solution.py:288
  74.6 34.1 %collective-permute-start.6 = (bf16[27,16,256]{2,1,0:T(8,128)(2,1)}, bf16[27,16,256]{2,1,0:T(8,128)(2,1)}, u32[]{:S(2)}, u32[]{:S(2)}) collective-permute-start(bf16[27,16,256]{2,1,0:T(8,128)(2,1)} %get-tuple-element.56), channel_id=1, source_target_pairs={{0,224},{2,226},{4,228},{6,230},{8,232},{10,234},{12,236},{14,238}... | collective-permute-start | bytes 663560 | tf_op jit(solution)/shard_map/cond/branch_1_fun/ppermute | solution.py:288
  108.7 8.4 %copy-start.26 = (bf16[25,16,256]{2,1,0:T(8,128)(2,1)S(1)}, bf16[25,16,256]{2,1,0:T(8,128)(2,1)}, u32[]{:S(2)}) copy-start(bf16[25,16,256]{2,1,0:T(8,128)(2,1)} %get-tuple-element.61) | copy-start | bytes 614404 | tf_op jit(solution)/shard_map/cond
  108.7 11.3 %copy-start.25 = (bf16[25,16,256]{2,1,0:T(8,128)(2,1)S(1)}, bf16[25,16,256]{2,1,0:T(8,128)(2,1)}, u32[]{:S(2)}) copy-start(bf16[25,16,256]{2,1,0:T(8,128)(2,1)} %get-tuple-element.62) | copy-start | bytes 614404 | tf_op jit(solution)/shard_map/cond
  113.3 51.0 %all-to-all-start.2 = ((bf16[16,15,16,256]{3,2,1,0:T(8,128)(2,1)}), bf16[16,15,16,256]{3,2,1,0:T(8,128)(2,1)S(1)}, u32[]{:S(2)}, u32[]{:S(2)}) async-start(bf16[16,15,16,256]{3,2,1,0:T(8,128)(2,1)} %bitcast.33), calls=%async_computation.2 | async-start | bytes 3932160 | tf_op jit(solution)/shard_map/cond/branch_1_fun/all_to_all | solution.py:302
  117.0 10.2 %collective-permute-start.10 = (bf16[25,16,256]{2,1,0:T(8,128)(2,1)S(1)}, bf16[25,16,256]{2,1,0:T(8,128)(2,1)S(1)}, u32[]{:S(2)}, u32[]{:S(2)}) collective-permute-start(bf16[25,16,256]{2,1,0:T(8,128)(2,1)S(1)} %copy-done.26), channel_id=1, source_target_pairs={{0,128},{2,130},{4,132},{6,134},{8,136},{10,138},{12,140},{14,142}... | collective-permute-start | bytes 614408 | tf_op jit(solution)/shard_map/cond/branch_1_fun/ppermute | solution.py:288
  120.0 25.2 %collective-permute-start.11 = (bf16[25,16,256]{2,1,0:T(8,128)(2,1)S(1)}, bf16[25,16,256]{2,1,0:T(8,128)(2,1)S(1)}, u32[]{:S(2)}, u32[]{:S(2)}) collective-permute-start(bf16[25,16,256]{2,1,0:T(8,128)(2,1)S(1)} %copy-done.25), channel_id=1, source_target_pairs={{0,160},{2,162},{4,164},{6,166},{8,168},{10,170},{12,172},{14,174}... | collective-permute-start | bytes 614408 | tf_op jit(solution)/shard_map/cond/branch_1_fun/ppermute | solution.py:288
  122.5 32.7 %collective-permute-start.12 = (bf16[25,16,256]{2,1,0:T(8,128)(2,1)}, bf16[25,16,256]{2,1,0:T(8,128)(2,1)S(1)}, u32[]{:S(2)}, u32[]{:S(2)}) collective-permute-start(bf16[25,16,256]{2,1,0:T(8,128)(2,1)} %get-tuple-element.63), channel_id=1, source_target_pairs={{0,192},{2,194},{4,196},{6,198},{8,200},{10,202},{12,204},{14,206}... | collective-permute-start | bytes 614408 | tf_op jit(solution)/shard_map/cond/branch_1_fun/ppermute | solution.py:288
  125.8 33.0 %collective-permute-start.13 = (bf16[25,16,256]{2,1,0:T(8,128)(2,1)}, bf16[25,16,256]{2,1,0:T(8,128)(2,1)S(1)}, u32[]{:S(2)}, u32[]{:S(2)}) collective-permute-start(bf16[25,16,256]{2,1,0:T(8,128)(2,1)} %get-tuple-element.64), channel_id=1, source_target_pairs={{0,224},{2,226},{4,228},{6,230},{8,232},{10,234},{12,236},{14,238}... | collective-permute-start | bytes 614408 | tf_op jit(solution)/shard_map/cond/branch_1_fun/ppermute | solution.py:288
  125.8 33.0 %collective-permute-start.7 = (bf16[25,16,256]{2,1,0:T(8,128)(2,1)}, bf16[25,16,256]{2,1,0:T(8,128)(2,1)S(1)}, u32[]{:S(2)}, u32[]{:S(2)}) collective-permute-start(bf16[25,16,256]{2,1,0:T(8,128)(2,1)} %get-tuple-element.58), channel_id=1, source_target_pairs={{0,32},{2,34},{4,36},{6,38},{8,40},{10,42},{12,44},{14,46},{16,48}... | collective-permute-start | bytes 614408 | tf_op jit(solution)/shard_map/cond/branch_1_fun/ppermute | solution.py:288
  127.3 31.6 %copy-start.4 = (bf16[25,16,256]{2,1,0:T(8,128)(2,1)}, bf16[25,16,256]{2,1,0:T(8,128)(2,1)S(1)}, u32[]{:S(2)}) copy-start(bf16[25,16,256]{2,1,0:T(8,128)(2,1)S(1)} %collective-permute-done.10.rest_4_) | copy-start | bytes 614404 | tf_op jit(solution)/shard_map/cond
  127.3 31.6 %collective-permute-start.8 = (bf16[25,16,256]{2,1,0:T(8,128)(2,1)}, bf16[25,16,256]{2,1,0:T(8,128)(2,1)S(1)}, u32[]{:S(2)}, u32[]{:S(2)}) collective-permute-start(bf16[25,16,256]{2,1,0:T(8,128)(2,1)} %get-tuple-element.59), channel_id=1, source_target_pairs={{0,64},{2,66},{4,68},{6,70},{8,72},{10,74},{12,76},{14,78},{16,80}... | collective-permute-start | bytes 614408 | tf_op jit(solution)/shard_map/cond/branch_1_fun/ppermute | solution.py:288
  145.2 13.6 %copy-start.5 = (bf16[25,16,256]{2,1,0:T(8,128)(2,1)}, bf16[25,16,256]{2,1,0:T(8,128)(2,1)S(1)}, u32[]{:S(2)}) copy-start(bf16[25,16,256]{2,1,0:T(8,128)(2,1)S(1)} %collective-permute-done.11.rest_5_) | copy-start | bytes 614404 | tf_op jit(solution)/shard_map/cond
  145.2 13.6 %collective-permute-start.9 = (bf16[25,16,256]{2,1,0:T(8,128)(2,1)}, bf16[25,16,256]{2,1,0:T(8,128)(2,1)S(1)}, u32[]{:S(2)}, u32[]{:S(2)}) collective-permute-start(bf16[25,16,256]{2,1,0:T(8,128)(2,1)} %get-tuple-element.60), channel_id=1, source_target_pairs={{0,96},{2,98},{4,100},{6,102},{8,104},{10,106},{12,108},{14,110},{... | collective-permute-start | bytes 614408 | tf_op jit(solution)/shard_map/cond/branch_1_fun/ppermute | solution.py:288
  164.3 9.1 %copy-start.32 = (bf16[15,16,256]{2,1,0:T(8,128)(2,1)S(1)}, bf16[15,16,256]{2,1,0:T(8,128)(2,1)}, u32[]{:S(2)}) copy-start(bf16[15,16,256]{2,1,0:T(8,128)(2,1)} %get-tuple-element.66) | copy-start | bytes 368644 | tf_op jit(solution)/shard_map/cond
  164.3 11.3 %copy-start.31 = (bf16[15,16,256]{2,1,0:T(8,128)(2,1)S(1)}, bf16[15,16,256]{2,1,0:T(8,128)(2,1)}, u32[]{:S(2)}) copy-start(bf16[15,16,256]{2,1,0:T(8,128)(2,1)} %get-tuple-element.67) | copy-start | bytes 368644 | tf_op jit(solution)/shard_map/cond
  164.3 17.0 %copy-start.30 = (bf16[15,16,256]{2,1,0:T(8,128)(2,1)S(1)}, bf16[15,16,256]{2,1,0:T(8,128)(2,1)}, u32[]{:S(2)}) copy-start(bf16[15,16,256]{2,1,0:T(8,128)(2,1)} %get-tuple-element.69) | copy-start | bytes 368644 | tf_op jit(solution)/shard_map/cond
  164.3 18.5 %copy-start.29 = (bf16[15,16,256]{2,1,0:T(8,128)(2,1)S(1)}, bf16[15,16,256]{2,1,0:T(8,128)(2,1)}, u32[]{:S(2)}) copy-start(bf16[15,16,256]{2,1,0:T(8,128)(2,1)} %get-tuple-element.70) | copy-start | bytes 368644 | tf_op jit(solution)/shard_map/cond
  164.3 21.2 %copy-start.28 = (bf16[15,16,256]{2,1,0:T(8,128)(2,1)S(1)}, bf16[15,16,256]{2,1,0:T(8,128)(2,1)}, u32[]{:S(2)}) copy-start(bf16[15,16,256]{2,1,0:T(8,128)(2,1)} %get-tuple-element.71) | copy-start | bytes 368644 | tf_op jit(solution)/shard_map/cond
  164.3 22.9 %copy-start.27 = (bf16[15,16,256]{2,1,0:T(8,128)(2,1)S(1)}, bf16[15,16,256]{2,1,0:T(8,128)(2,1)}, u32[]{:S(2)}) copy-start(bf16[15,16,256]{2,1,0:T(8,128)(2,1)} %get-tuple-element.72) | copy-start | bytes 368644 | tf_op jit(solution)/shard_map/cond
  164.4 46.0 %copy-start = (bf16[16,15,16,256]{3,2,1,0:T(8,128)(2,1)}, bf16[16,15,16,256]{3,2,1,0:T(8,128)(2,1)S(1)}, u32[]{:S(2)}) copy-start(bf16[16,15,16,256]{3,2,1,0:T(8,128)(2,1)S(1)} %all-to-all-done.2) | copy-start | bytes 5898244 | tf_op jit(solution)/shard_map/cond
  164.4 45.9 %all-to-all-start.1 = ((bf16[16,15,16,256]{3,2,1,0:T(8,128)(2,1)}), bf16[16,15,16,256]{3,2,1,0:T(8,128)(2,1)}, u32[]{:S(2)}, u32[]{:S(2)}) async-start(bf16[16,15,16,256]{3,2,1,0:T(8,128)(2,1)} %bitcast.35), calls=%async_computation.1 | async-start | bytes 3932160 | tf_op jit(solution)/shard_map/cond/branch_1_fun/all_to_all | solution.py:302
  173.3 12.2 %collective-permute-start.14 = (bf16[15,16,256]{2,1,0:T(8,128)(2,1)S(1)}, bf16[15,16,256]{2,1,0:T(8,128)(2,1)S(1)}, u32[]{:S(2)}, u32[]{:S(2)}) collective-permute-start(bf16[15,16,256]{2,1,0:T(8,128)(2,1)S(1)} %copy-done.32), channel_id=1, source_target_pairs={{0,32},{2,34},{4,36},{6,38},{8,40},{10,42},{12,44},{14,46},{16,48}... | collective-permute-start | bytes 368648 | tf_op jit(solution)/shard_map/cond/branch_1_fun/ppermute | solution.py:288
  175.6 11.6 %collective-permute-start.15 = (bf16[15,16,256]{2,1,0:T(8,128)(2,1)S(1)}, bf16[15,16,256]{2,1,0:T(8,128)(2,1)S(1)}, u32[]{:S(2)}, u32[]{:S(2)}) collective-permute-start(bf16[15,16,256]{2,1,0:T(8,128)(2,1)S(1)} %copy-done.31), channel_id=1, source_target_pairs={{0,64},{2,66},{4,68},{6,70},{8,72},{10,74},{12,76},{14,78},{16,80}... | collective-permute-start | bytes 368648 | tf_op jit(solution)/shard_map/cond/branch_1_fun/ppermute | solution.py:288
  179.3 19.7 %collective-permute-start.16 = (bf16[15,16,256]{2,1,0:T(8,128)(2,1)}, bf16[15,16,256]{2,1,0:T(8,128)(2,1)S(1)}, u32[]{:S(2)}, u32[]{:S(2)}) collective-permute-start(bf16[15,16,256]{2,1,0:T(8,128)(2,1)} %get-tuple-element.68), channel_id=1, source_target_pairs={{0,96},{2,98},{4,100},{6,102},{8,104},{10,106},{12,108},{14,110},{... | collective-permute-start | bytes 368648 | tf_op jit(solution)/shard_map/cond/branch_1_fun/ppermute | solution.py:288
  181.3 17.8 %collective-permute-start.17 = (bf16[15,16,256]{2,1,0:T(8,128)(2,1)S(1)}, bf16[15,16,256]{2,1,0:T(8,128)(2,1)S(1)}, u32[]{:S(2)}, u32[]{:S(2)}) collective-permute-start(bf16[15,16,256]{2,1,0:T(8,128)(2,1)S(1)} %copy-done.30), channel_id=1, source_target_pairs={{0,128},{2,130},{4,132},{6,134},{8,136},{10,138},{12,140},{14,142}... | collective-permute-start | bytes 368648 | tf_op jit(solution)/shard_map/cond/branch_1_fun/ppermute | solution.py:288
  182.8 16.2 %collective-permute-start.18 = (bf16[15,16,256]{2,1,0:T(8,128)(2,1)S(1)}, bf16[15,16,256]{2,1,0:T(8,128)(2,1)S(1)}, u32[]{:S(2)}, u32[]{:S(2)}) collective-permute-start(bf16[15,16,256]{2,1,0:T(8,128)(2,1)S(1)} %copy-done.29), channel_id=1, source_target_pairs={{0,160},{2,162},{4,164},{6,166},{8,168},{10,170},{12,172},{14,174}... | collective-permute-start | bytes 368648 | tf_op jit(solution)/shard_map/cond/branch_1_fun/ppermute | solution.py:288
  185.5 21.1 %copy-start.11 = (bf16[15,16,256]{2,1,0:T(8,128)(2,1)}, bf16[15,16,256]{2,1,0:T(8,128)(2,1)S(1)}, u32[]{:S(2)}) copy-start(bf16[15,16,256]{2,1,0:T(8,128)(2,1)S(1)} %collective-permute-done.14.rest_1_) | copy-start | bytes 368644 | tf_op jit(solution)/shard_map/cond
  185.6 18.5 %collective-permute-start.19 = (bf16[15,16,256]{2,1,0:T(8,128)(2,1)S(1)}, bf16[15,16,256]{2,1,0:T(8,128)(2,1)S(1)}, u32[]{:S(2)}, u32[]{:S(2)}) collective-permute-start(bf16[15,16,256]{2,1,0:T(8,128)(2,1)S(1)} %copy-done.28), channel_id=1, source_target_pairs={{0,192},{2,194},{4,196},{6,198},{8,200},{10,202},{12,204},{14,206}... | collective-permute-start | bytes 368648 | tf_op jit(solution)/shard_map/cond/branch_1_fun/ppermute | solution.py:288
  187.2 19.5 %copy-start.12 = (bf16[15,16,256]{2,1,0:T(8,128)(2,1)}, bf16[15,16,256]{2,1,0:T(8,128)(2,1)S(1)}, u32[]{:S(2)}) copy-start(bf16[15,16,256]{2,1,0:T(8,128)(2,1)S(1)} %collective-permute-done.15.rest_2_) | copy-start | bytes 368644 | tf_op jit(solution)/shard_map/cond
  187.2 19.4 %collective-permute-start.20 = (bf16[15,16,256]{2,1,0:T(8,128)(2,1)S(1)}, bf16[15,16,256]{2,1,0:T(8,128)(2,1)S(1)}, u32[]{:S(2)}, u32[]{:S(2)}) collective-permute-start(bf16[15,16,256]{2,1,0:T(8,128)(2,1)S(1)} %copy-done.27), channel_id=1, source_target_pairs={{0,224},{2,226},{4,228},{6,230},{8,232},{10,234},{12,236},{14,238}... | collective-permute-start | bytes 368648 | tf_op jit(solution)/shard_map/cond/branch_1_fun/ppermute | solution.py:288
  210.3 27.8 %all-to-all-start = ((bf16[16,12,16,256]{3,2,1,0:T(8,128)(2,1)}), bf16[16,12,16,256]{3,2,1,0:T(8,128)(2,1)}, u32[]{:S(2)}, u32[]{:S(2)}) async-start(bf16[16,12,16,256]{3,2,1,0:T(8,128)(2,1)} %bitcast.36), calls=%async_computation | async-start | bytes 3145728 | tf_op jit(solution)/shard_map/cond/branch_1_fun/all_to_all | solution.py:302
  (16 other events, 53.7 us)
